TPU v7x, 32 devices: a whole 2x2x4 slice. The times are simulated.
32 devices in a mesh: dp: 4 (over x, core), tensor: 8 (over z, y).
Axes of the slice: x: 2, y: 2, z: 4, core: 2. Of those that a mesh axis runs over, the one named last changes fastest.
Arguments:
- out_grad: bfloat16 [2, 320, 4096], P(None, 'dp', 'tensor'), may hold values from -0.3125 to 0.3125
- layer_input: bfloat16 [2, 320, 4096], P(None, 'dp', 'tensor'), may hold values from -8 to 8
- w_down: bfloat16 [16384, 4096], P('tensor'), may hold values from -0.046875 to 0.046875
- silu_gate: bfloat16 [2, 320, 16384], P(None, 'dp', 'tensor'), may hold values from -6 to 6
- up_proj: bfloat16 [2, 320, 16384], P(None, 'dp', 'tensor'), may hold values from -6 to 6
- slope_codes: int32 [2, 32, 16384], P(None, 'dp', 'tensor'), may hold values from 0 to 1073741823
Outputs:
- grad_down: bfloat16 [16384, 4096], P('tensor', 'dp')
- grad_gate: bfloat16 [4096, 16384], P('dp', 'tensor')
- grad_up: bfloat16 [4096, 16384], P('dp', 'tensor')
Inputs may be any that keep to these rules, and one draw needn't show every extreme that they name: `slope_codes`: every word holds ten independent 3-bit codes; all eight codes occur.
All inputs are finite; a program needn't handle non-finite values.
Results may differ from a plain program's by a relative error of at most 0.018.
Values may be sent and summed in bfloat16 or wider, within the bound.
A program may use at most 128 MiB of HBM per device.

v0:
```python
import jax
import jax.numpy as jnp
from jax import lax
from jax.sharding import PartitionSpec as P

SLOPE_LEVELS = (-0.09, 0.06, 0.22, 0.41, 0.6, 0.79, 0.96, 1.08)


def decode_slopes(packed):
    shifts = 3 * jnp.arange(10, dtype=jnp.int32)
    pieces = jnp.bitwise_and(jnp.right_shift(packed[..., None, :], shifts[:, None]), 7)
    pieces = pieces.reshape(packed.shape[:-2] + (packed.shape[-2] * 10, packed.shape[-1]))
    result = jnp.full(pieces.shape, SLOPE_LEVELS[0], jnp.float32)
    for symbol in range(1, 8):
        result = jnp.where(pieces == symbol, jnp.float32(SLOPE_LEVELS[symbol]), result)
    return result


def shards(out_grad, layer_input, w_down, silu_gate, up_proj, slope_codes):
    micro_count = out_grad.shape[0]
    model_width = w_down.shape[1]
    hidden_width = w_down.shape[0]
    group_rows = micro_count * out_grad.shape[1]
    grad_rows, input_rows = (
        lax.all_gather(out_grad, "tensor", axis=2, tiled=True),
        lax.all_gather(layer_input, "tensor", axis=2, tiled=True),
    )
    output_all = grad_rows.reshape(-1, model_width)
    input_all = input_rows.reshape(-1, model_width)
    gate_act = silu_gate.reshape(-1, hidden_width).astype(jnp.float32)
    up_value = up_proj.reshape(-1, hidden_width).astype(jnp.float32)
    hidden = (gate_act * up_value).astype(jnp.bfloat16)
    slopes = decode_slopes(slope_codes).reshape(-1, hidden_width)
    hidden_grad = lax.dot_general(
        output_all, w_down, (((1,), (1,)), ((), ())), preferred_element_type=jnp.float32
    )
    up_grad = (hidden_grad * gate_act).astype(jnp.bfloat16)
    gate_grad = (hidden_grad * up_value * slopes).astype(jnp.bfloat16)
    block_inputs, block_outputs = (
        lax.all_to_all(input_all, "dp", split_axis=1, concat_axis=0, tiled=True),
        lax.all_to_all(output_all, "dp", split_axis=1, concat_axis=0, tiled=True),
    )
    activations = jnp.concatenate((gate_grad, up_grad, hidden), axis=1)
    values = lax.all_gather(activations, "dp", axis=0, tiled=True)
    row_count = values.shape[0]
    groups = row_count // group_rows
    inputs_3d = block_inputs.reshape(groups, group_rows, block_inputs.shape[1])
    outputs_3d = block_outputs.reshape(groups, group_rows, block_outputs.shape[1])
    values_3d = values.reshape(groups, group_rows, values.shape[1])
    gate_up_parts = jnp.einsum(
        "grd,grf->gdf",
        inputs_3d,
        values_3d[:, :, : 2 * hidden_width],
        preferred_element_type=jnp.float32,
    )
    down_parts = jnp.einsum(
        "grf,grd->gfd",
        values_3d[:, :, 2 * hidden_width :],
        outputs_3d,
        preferred_element_type=jnp.float32,
    )
    gate_up_sum = jnp.sum(gate_up_parts.astype(jnp.bfloat16).astype(jnp.float32), axis=0)
    down_sum = jnp.sum(down_parts.astype(jnp.bfloat16).astype(jnp.float32), axis=0)
    grad_down = down_sum.astype(jnp.bfloat16)
    grad_gate = gate_up_sum[:, :hidden_width].astype(jnp.bfloat16)
    grad_up = gate_up_sum[:, hidden_width:].astype(jnp.bfloat16)
    return (grad_down, grad_gate, grad_up)


def solution(mesh):
    return jax.shard_map(
        shards,
        mesh=mesh,
        in_specs=(
            P(None, "dp", "tensor"),
            P(None, "dp", "tensor"),
            P("tensor", None),
            P(None, "dp", "tensor"),
            P(None, "dp", "tensor"),
            P(None, "dp", "tensor"),
        ),
        out_specs=(P("tensor", "dp"), P("dp", "tensor"), P("dp", "tensor")),
        check_vma=False,
    )
```

profile of v0, /device:TPU:0, one launch (start us, length us, event | category | flops | bytes accessed | tf_op | source)
XLA Modules:
  0.0 234.2 jit_solution(13841438188736707465)
XLA Ops:
  7.2 0.0 all-gather.4.cloned.1.call-start
  7.2 0.7 all-gather.4.cloned.1.call-update
  7.9 0.0 all-gather.8.cloned.1.call-start
  7.9 0.7 all-gather.8.cloned.1.call-update
  8.6 0.0 all-gather.6.cloned.1.call-start
  8.7 0.1 shift_right_arithmetic.28
  8.8 0.1 shift_right_arithmetic.30
  8.9 1.1 shift_right_arithmetic.25
  10.0 0.2 shift_right_arithmetic.26
  10.2 44.1 %all-gather.4.cloned.1.call-done = bf16[2,80,4096]{2,1,0:T(8,128)(2,1)} async-done(((bf16[2,80,512]{2,1,0:T(8,128)(2,1)}), bf16[2,80,4096]{2,1,0:T(8,128)(2,1)}) %all-gather.4.cloned.1.call-update) | async-done | bytes 1310736 | tf_op jit(solution)/shard_map/all_gather | solution.py:25
  54.3 12.8 %fusion.4 = (bf16[160,2048]{1,0:T(8,128)(2,1)S(1)}, bf16[160,2048]{1,0:T(8,128)(2,1)S(1)}, bf16[160,2048]{1,0:T(8,128)(2,1)S(1)}) fusion(s32[160,2048]{1,0:T(8,128)S(1)} %shift_right_arithmetic.26, bf16[2,80,2048]{2,1,0:T(8,128)(2,1)} %param.10, s32[160]{0:T(256)S(1)} %shift_right_arithmetic.30, bf16[2,80,2048]{2,1,0:T(8,128)(2,1)} %param.9, ...), kind=kOutput, calls=%fused_computation.10 | convolution fusion | flops 2692546560 | bytes 22676096 | tf_op jit(solution)/shard_map/dot_general | solution.py:34
  67.1 1.4 pad_maximum_fusion
  68.5 0.0 all-gather.6.cloned.1.call-update
  68.5 27.8 %all-gather.8.cloned.1.call-done = bf16[2,80,4096]{2,1,0:T(8,128)(2,1)} async-done(((bf16[2,80,512]{2,1,0:T(8,128)(2,1)}), bf16[2,80,4096]{2,1,0:T(8,128)(2,1)}) %all-gather.8.cloned.1.call-update) | async-done | bytes 1310736 | tf_op jit(solution)/shard_map/all_gather | solution.py:26
  96.3 3.2 %all_to_all.27 = bf16[160,4,1024]{2,1,0:T(4,128)(2,1)S(1)} reshape(bf16[2,80,4096]{2,1,0:T(8,128)(2,1)} %all-gather.8.cloned.1.call-done) | data formatting | bytes 2621440 | tf_op jit(solution)/shard_map/all_to_all | solution.py:40
  99.5 1.4 copy.12
  101.0 0.0 copy-start
  101.0 4.5 %all-to-all-start.1 = ((bf16[160,4,1024]{2,0,1:T(8,128)(2,1)}), bf16[160,4,1024]{2,0,1:T(8,128)(2,1)}, u32[]{:S(2)}, u32[]{:S(2)}) async-start(bf16[160,4,1024]{2,0,1:T(8,128)(2,1)} %copy.12), calls=%async_computation.1 | async-start | bytes 2621440 | tf_op jit(solution)/shard_map/all_to_all | solution.py:40
  105.5 0.0 copy-done
  105.5 1.0 all_to_all.24
  106.5 1.5 copy.11
  108.0 29.0 %all-to-all-done.1 = bf16[160,4,1024]{2,0,1:T(8,128)(2,1)} async-done(((bf16[160,4,1024]{2,0,1:T(8,128)(2,1)}), bf16[160,4,1024]{2,0,1:T(8,128)(2,1)}, u32[]{:S(2)}, u32[]{:S(2)}) %all-to-all-start.1) | async-done | bytes 1310752 | tf_op jit(solution)/shard_map/all_to_all | solution.py:40
  137.0 3.7 %all-to-all-start = ((bf16[160,4,1024]{2,0,1:T(8,128)(2,1)}), bf16[160,4,1024]{2,0,1:T(8,128)(2,1)S(1)}, u32[]{:S(2)}, u32[]{:S(2)}) async-start(bf16[160,4,1024]{2,0,1:T(8,128)(2,1)} %copy.11), calls=%async_computation | async-start | bytes 2621440 | tf_op jit(solution)/shard_map/all_to_all | solution.py:41
  140.8 39.4 %all-gather.6.cloned.1.call-done = bf16[640,6144]{1,0:T(8,128)(2,1)} async-done(((bf16[160,6144]{1,0:T(8,128)(2,1)}), bf16[640,6144]{1,0:T(8,128)(2,1)}) %all-gather.6.cloned.1.call-update) | async-done | bytes 7864336 | tf_op jit(solution)/shard_map/all_gather | solution.py:44
  180.2 19.0 %convert_reduce_fusion = bf16[4096,1024]{1,0:T(8,128)(2,1)} fusion(bf16[4,160,6144]{2,1,0:T(8,128)(2,1)} %bitcast.21, bf16[160,4,1024]{2,0,1:T(8,128)(2,1)} %all-to-all-done.1), kind=kOutput, calls=%fused_computation | convolution fusion | flops 5398069248 | bytes 14942208 | tf_op jit(solution)/shard_map/grd,grf->gdf/dot_general | solution.py:50
  199.2 6.0 %fusion.8 = (bf16[1024,2048]{0,1:T(8,128)(2,1)}, bf16[1024,2048]{0,1:T(8,128)(2,1)}) fusion(bf16[1024,4096]{0,1:T(8,128)(2,1)} %bitcast.19), kind=kLoop, calls=%fused_computation.16 | loop fusion | bytes 16777216 | tf_op jit(solution)/shard_map/slice | solution.py:66
  205.2 6.4 %copy.14 = bf16[1024,2048]{1,0:T(8,128)(2,1)} copy(bf16[1024,2048]{0,1:T(8,128)(2,1)} %get-tuple-element.6) | data formatting | bytes 8388608
  211.6 6.4 %copy.13 = bf16[1024,2048]{1,0:T(8,128)(2,1)} copy(bf16[1024,2048]{0,1:T(8,128)(2,1)} %get-tuple-element.7) | data formatting | bytes 8388608
  218.0 0.0 all-to-all-done
  218.0 9.6 %convert_reduce_fusion.1 = bf16[2048,1024]{1,0:T(8,128)(2,1)} fusion(bf16[4,160,6144]{2,1,0:T(8,128)(2,1)} %bitcast.22, bf16[160,4,1024]{2,0,1:T(8,128)(2,1)S(1)} %all-to-all-done), kind=kOutput, calls=%fused_computation.1 | convolution fusion | flops 2699034624 | bytes 8126464 | tf_op jit(solution)/shard_map/grf,grd->gfd/dot_general | solution.py:56
  (3 shorter events, 0.0 us)
Async XLA Ops:
  7.2 47.2 %all-gather.4.cloned.1.call-start = ((), (), s32[]{:S(2)}) async-start(), calls=%async_computation.2 | async-start | bytes 1474560 | tf_op jit(solution)/shard_map/all_gather | solution.py:25
  7.9 88.4 %all-gather.8.cloned.1.call-start = ((), (), s32[]{:S(2)}) async-start(), calls=%async_computation.4 | async-start | bytes 1474560 | tf_op jit(solution)/shard_map/all_gather | solution.py:26
  8.6 171.5 %all-gather.6.cloned.1.call-start = ((), (), s32[]{:S(2)}) async-start(), calls=%async_computation.3 | async-start | bytes 9830400 | tf_op jit(solution)/shard_map/all_gather | solution.py:44
  101.0 4.5 %copy-start = (bf16[2,80,4096]{2,1,0:T(8,128)(2,1)S(1)}, bf16[2,80,4096]{2,1,0:T(8,128)(2,1)}, u32[]{:S(2)}) copy-start(bf16[2,80,4096]{2,1,0:T(8,128)(2,1)} %all-gather.4.cloned.1.call-done) | copy-start | bytes 3932164
  101.0 36.0 %all-to-all-start.1 = ((bf16[160,4,1024]{2,0,1:T(8,128)(2,1)}), bf16[160,4,1024]{2,0,1:T(8,128)(2,1)}, u32[]{:S(2)}, u32[]{:S(2)}) async-start(bf16[160,4,1024]{2,0,1:T(8,128)(2,1)} %copy.12), calls=%async_computation.1 | async-start | bytes 2621440 | tf_op jit(solution)/shard_map/all_to_all | solution.py:40
  137.0 81.0 %all-to-all-start = ((bf16[160,4,1024]{2,0,1:T(8,128)(2,1)}), bf16[160,4,1024]{2,0,1:T(8,128)(2,1)S(1)}, u32[]{:S(2)}, u32[]{:S(2)}) async-start(bf16[160,4,1024]{2,0,1:T(8,128)(2,1)} %copy.11), calls=%async_computation | async-start | bytes 2621440 | tf_op jit(solution)/shard_map/all_to_all | solution.py:41
Sparse Core Ops, SparseCore 0:
  10.0 44.2 all-gather.3
  56.4 39.8 all-gather.7
  98.4 81.6 all-gather.5
where the time goes:
time: 235 us; the launch traced here: 234 us
  waiting for transfers between devices  142 us (60%)
  matrix products  41.4 us (18%)
  local copies, waits for them, and re-layouts  27.5 us (12%)
  between operations  13.8 us (6%)
  starting transfers between devices  8.34 us (4%)
    all_gather x1, waiting for transfers between devices, shards(): lax.all_gather(out_grad, 'tensor', axis=2, tiled=True)  44.1 us
    all_gather x1, waiting for transfers between devices, shards(): values = lax.all_gather(activations, 'dp', axis=0, tiled=True)  39.4 us
    all_to_all x1, waiting for transfers between devices, shards(): lax.all_to_all(input_all, 'dp', split_axis=1, concat_axis=0, tiled=True)  29 us
    all_gather x1, waiting for transfers between devices, shards(): lax.all_gather(layer_input, 'tensor', axis=2, tiled=True)  27.8 us
    dot_general x1, matrix products, shards(): jnp.einsum('grd,grf->gdf', inputs_3d, values_3d[:, :, :2 * hidden_width],...  19 us
    unnamed x4, local copies, waits for them, and re-layouts  12.8 us
    dot_general x1, matrix products, shards(): lax.dot_general(output_all, w_down, (((1,), (1,)), ((), ())), preferred_e...  12.8 us
    dot_general x1, matrix products, shards(): jnp.einsum('grf,grd->gfd', values_3d[:, :, 2 * hidden_width:], outputs_3d...  9.61 us
  transfers between devices with their start and end apart: 5, of which 4 were waited for; matrix products, arithmetic and copies ran while one was open for 24% of the time, Pallas kernels for 0%

commit v1 on v0

--- a/solution.py
+++ b/solution.py
@@ -37,7 +37,12 @@
     up_grad = (hidden_grad * gate_act).astype(jnp.bfloat16)
     gate_grad = (hidden_grad * up_value * slopes).astype(jnp.bfloat16)
     block_inputs, block_outputs = (
-        lax.all_to_all(input_all, "dp", split_axis=1, concat_axis=0, tiled=True),
+        jnp.concatenate(
+            lax.all_to_all(
+                jnp.stack(jnp.split(input_all, lax.axis_size("dp"), axis=1)), "dp", 0, 0
+            ),
+            axis=0,
+        ),
         lax.all_to_all(output_all, "dp", split_axis=1, concat_axis=0, tiled=True),
     )
     activations = jnp.concatenate((gate_grad, up_grad, hidden), axis=1)

time: 235 us -> 228 us (0.970)
  local copies, waits for them, and re-layouts: 27.5 us -> 11.5 us
  matrix products: 41.4 us -> 49.1 us
    unnamed x4 -> x2, local copies, waits for them, and re-layouts: 12.8 us -> 0.01 us
    dot_general x1, matrix products: 19 us -> 26.8 us  [shards(): jnp.einsum('grd,grf->gdf', inputs_3d, values_3d[:, :, :2 * hidden_width],...]
    all_to_all x2 -> x0, local copies, waits for them, and re-layouts: 4.67 us -> none  [shards(): lax.all_to_all(input_all, 'dp', split_axis=1, concat_axis=0, tiled=True)]
  transfers between devices with their start and end apart: 5 -> 5, of which waited for: 4 -> 4; matrix products, arithmetic and copies ran while one was open for 24% -> 23% of each run, Pallas kernels for 0% -> 0%
where the time goes in v1:
time: 228 us
  waiting for transfers between devices  142 us (62%)
  matrix products  49.1 us (22%)
  between operations  13.8 us (6%)
  local copies, waits for them, and re-layouts  11.5 us (5%)
  starting transfers between devices  8.27 us (4%)
  other arithmetic  2.63 us (1%)
    all_gather x1, waiting for transfers between devices, shards(): lax.all_gather(out_grad, 'tensor', axis=2, tiled=True)  44.1 us
    all_gather x1, waiting for transfers between devices, shards(): values = lax.all_gather(activations, 'dp', axis=0, tiled=True)  41.2 us
    all_gather x1, waiting for transfers between devices, shards(): lax.all_gather(layer_input, 'tensor', axis=2, tiled=True)  27.8 us
    all_to_all x1, waiting for transfers between devices, shards(): lax.all_to_all(jnp.stack(jnp.split(input_all, lax.axis_size('dp'), axis=1...  27.7 us
    dot_general x1, matrix products, shards(): jnp.einsum('grd,grf->gdf', inputs_3d, values_3d[:, :, :2 * hidden_width],...  26.8 us
    dot_general x1, matrix products, shards(): lax.dot_general(output_all, w_down, (((1,), (1,)), ((), ())), preferred_e...  12.8 us
    dot_general x1, matrix products, shards(): jnp.einsum('grf,grd->gfd', values_3d[:, :, 2 * hidden_width:], outputs_3d...  9.61 us
    slice x1, local copies, waits for them, and re-layouts, shards(): grad_up = gate_up_sum[:, hidden_width:].astype(jnp.bfloat16)  6.14 us
  transfers between devices with their start and end apart: 5, of which 4 were waited for; matrix products, arithmetic and copies ran while one was open for 23% of the time, Pallas kernels for 0%

profile of v1, /device:TPU:0, one launch (start us, length us, event | category | flops | bytes accessed | tf_op | source)
XLA Modules:
  0.0 227.5 jit_solution(3306116674054740505)
XLA Ops:
  7.2 0.0 all-gather.4.cloned.1.call-start
  7.2 0.7 all-gather.4.cloned.1.call-update
  7.9 0.0 all-gather.8.cloned.1.call-start
  7.9 0.7 all-gather.8.cloned.1.call-update
  8.6 0.0 all-gather.6.cloned.1.call-start
  8.7 0.1 shift_right_arithmetic.28
  8.8 0.1 shift_right_arithmetic.30
  8.9 1.1 shift_right_arithmetic.25
  10.0 0.2 shift_right_arithmetic.26
  10.2 44.1 %all-gather.4.cloned.1.call-done = bf16[2,80,4096]{2,1,0:T(8,128)(2,1)} async-done(((bf16[2,80,512]{2,1,0:T(8,128)(2,1)}), bf16[2,80,4096]{2,1,0:T(8,128)(2,1)}) %all-gather.4.cloned.1.call-update) | async-done | bytes 1310736 | tf_op jit(solution)/shard_map/all_gather | solution.py:25
  54.3 12.8 %fusion.4 = (bf16[160,2048]{1,0:T(8,128)(2,1)S(1)}, bf16[160,2048]{1,0:T(8,128)(2,1)S(1)}, bf16[160,2048]{1,0:T(8,128)(2,1)S(1)}) fusion(s32[160,2048]{1,0:T(8,128)S(1)} %shift_right_arithmetic.26, bf16[2,80,2048]{2,1,0:T(8,128)(2,1)} %param.10, s32[160]{0:T(256)S(1)} %shift_right_arithmetic.30, bf16[2,80,2048]{2,1,0:T(8,128)(2,1)} %param.9, ...), kind=kOutput, calls=%fused_computation.10 | convolution fusion | flops 2692546560 | bytes 22676096 | tf_op jit(solution)/shard_map/dot_general | solution.py:34
  67.1 1.4 pad_maximum_fusion
  68.5 0.0 all-gather.6.cloned.1.call-update
  68.5 27.8 %all-gather.8.cloned.1.call-done = bf16[2,80,4096]{2,1,0:T(8,128)(2,1)} async-done(((bf16[2,80,512]{2,1,0:T(8,128)(2,1)}), bf16[2,80,4096]{2,1,0:T(8,128)(2,1)}) %all-gather.8.cloned.1.call-update) | async-done | bytes 1310736 | tf_op jit(solution)/shard_map/all_gather | solution.py:26
  96.3 1.4 slice_bitcast_fusion.3
  97.7 1.2 pad_maximum_fusion.1
  98.9 0.0 copy-start
  98.9 4.4 %all-to-all-start.1 = ((bf16[4,160,1024]{2,1,0:T(8,128)(2,1)}), bf16[4,160,1024]{2,1,0:T(8,128)(2,1)}, u32[]{:S(2)}, u32[]{:S(2)}) async-start(bf16[4,160,1024]{2,1,0:T(8,128)(2,1)} %pad_maximum_fusion.1), calls=%async_computation.1 | async-start | bytes 2621440 | tf_op jit(solution)/shard_map/all_to_all | solution.py:41
  103.3 0.0 copy-done
  103.3 1.0 all_to_all.15
  104.4 1.4 copy.9
  105.8 27.7 %all-to-all-done.1 = bf16[4,160,1024]{2,1,0:T(8,128)(2,1)} async-done(((bf16[4,160,1024]{2,1,0:T(8,128)(2,1)}), bf16[4,160,1024]{2,1,0:T(8,128)(2,1)}, u32[]{:S(2)}, u32[]{:S(2)}) %all-to-all-start.1) | async-done | bytes 1310752 | tf_op jit(solution)/shard_map/all_to_all | solution.py:41
  133.5 3.7 %all-to-all-start = ((bf16[160,4,1024]{2,0,1:T(8,128)(2,1)}), bf16[160,4,1024]{2,0,1:T(8,128)(2,1)S(1)}, u32[]{:S(2)}, u32[]{:S(2)}) async-start(bf16[160,4,1024]{2,0,1:T(8,128)(2,1)} %copy.9), calls=%async_computation | async-start | bytes 2621440 | tf_op jit(solution)/shard_map/all_to_all | solution.py:46
  137.2 41.2 %all-gather.6.cloned.1.call-done = bf16[640,6144]{1,0:T(8,128)(2,1)} async-done(((bf16[160,6144]{1,0:T(8,128)(2,1)}), bf16[640,6144]{1,0:T(8,128)(2,1)}) %all-gather.6.cloned.1.call-update) | async-done | bytes 7864336 | tf_op jit(solution)/shard_map/all_gather | solution.py:49
  178.5 26.8 %convert_reduce_fusion = bf16[1024,4096]{1,0:T(8,128)(2,1)} fusion(bf16[4,160,1024]{2,1,0:T(8,128)(2,1)} %all-to-all-done.1, bf16[4,160,6144]{2,1,0:T(8,128)(2,1)} %bitcast.27), kind=kOutput, calls=%fused_computation | convolution fusion | flops 5398069248 | bytes 14942208 | tf_op jit(solution)/shard_map/grd,grf->gdf/dot_general | solution.py:55
  205.3 6.1 %fusion.7 = (bf16[1024,2048]{1,0:T(8,128)(2,1)}, bf16[1024,2048]{1,0:T(8,128)(2,1)}) fusion(bf16[1024,4096]{1,0:T(8,128)(2,1)} %convert_reduce_fusion), kind=kLoop, calls=%fused_computation.20 | loop fusion | bytes 16777216 | tf_op jit(solution)/shard_map/slice | solution.py:71
  211.4 0.0 all-to-all-done
  211.4 9.6 %convert_reduce_fusion.1 = bf16[2048,1024]{1,0:T(8,128)(2,1)} fusion(bf16[4,160,6144]{2,1,0:T(8,128)(2,1)} %bitcast.28, bf16[160,4,1024]{2,0,1:T(8,128)(2,1)S(1)} %all-to-all-done), kind=kOutput, calls=%fused_computation.1 | convolution fusion | flops 2699034624 | bytes 8126464 | tf_op jit(solution)/shard_map/grf,grd->gfd/dot_general | solution.py:61
  (3 shorter events, 0.0 us)
Async XLA Ops:
  7.2 47.2 %all-gather.4.cloned.1.call-start = ((), (), s32[]{:S(2)}) async-start(), calls=%async_computation.2 | async-start | bytes 1474560 | tf_op jit(solution)/shard_map/all_gather | solution.py:25
  7.9 88.4 %all-gather.8.cloned.1.call-start = ((), (), s32[]{:S(2)}) async-start(), calls=%async_computation.4 | async-start | bytes 1474560 | tf_op jit(solution)/shard_map/all_gather | solution.py:26
  8.6 169.8 %all-gather.6.cloned.1.call-start = ((), (), s32[]{:S(2)}) async-start(), calls=%async_computation.3 | async-start | bytes 9830400 | tf_op jit(solution)/shard_map/all_gather | solution.py:49
  98.9 4.4 %copy-start = (bf16[2,80,4096]{2,1,0:T(8,128)(2,1)S(1)}, bf16[2,80,4096]{2,1,0:T(8,128)(2,1)}, u32[]{:S(2)}) copy-start(bf16[2,80,4096]{2,1,0:T(8,128)(2,1)} %all-gather.4.cloned.1.call-done) | copy-start | bytes 3932164
  98.9 34.6 %all-to-all-start.1 = ((bf16[4,160,1024]{2,1,0:T(8,128)(2,1)}), bf16[4,160,1024]{2,1,0:T(8,128)(2,1)}, u32[]{:S(2)}, u32[]{:S(2)}) async-start(bf16[4,160,1024]{2,1,0:T(8,128)(2,1)} %pad_maximum_fusion.1), calls=%async_computation.1 | async-start | bytes 2621440 | tf_op jit(solution)/shard_map/all_to_all | solution.py:41
  133.5 77.9 %all-to-all-start = ((bf16[160,4,1024]{2,0,1:T(8,128)(2,1)}), bf16[160,4,1024]{2,0,1:T(8,128)(2,1)S(1)}, u32[]{:S(2)}, u32[]{:S(2)}) async-start(bf16[160,4,1024]{2,0,1:T(8,128)(2,1)} %copy.9), calls=%async_computation | async-start | bytes 2621440 | tf_op jit(solution)/shard_map/all_to_all | solution.py:46
Sparse Core Ops, SparseCore 0:
  10.0 44.2 all-gather.3
  56.4 39.8 all-gather.7
  98.4 79.9 all-gather.5
